TPU v7x, 32 devices: a 4x4x1 block of a 4x4x8 slice. The times are simulated.
32 devices in a mesh: data: 1 (over z), model: 4 (over y), beam: 8 (over x, core).
Axes of the slice: x: 4, y: 4, z: 1, core: 2. Of those that a mesh axis runs over, the one named last changes fastest.
The devices are a block of a 4x4x8 slice.
Arguments:
- x_embed: bfloat16 [32, 4096], P(('data', 'beam'))
- parent: int32 [1, 32], P('data')
- position: int32 [], replicated
- score: float32 [32], P(('data', 'beam'))
- k_cache: bfloat16 [1, 32, 512, 32, 128], P(None, ('data', 'beam'), None, 'model')
- v_cache: bfloat16 [1, 32, 512, 32, 128], P(None, ('data', 'beam'), None, 'model')
- gain_attn: bfloat16 [1, 4096], replicated
- w_query: bfloat16 [1, 4096, 4096], P(None, None, 'model')
- w_key: bfloat16 [1, 4096, 4096], P(None, None, 'model')
- w_value: bfloat16 [1, 4096, 4096], P(None, None, 'model')
- w_out: bfloat16 [1, 4096, 4096], P(None, 'model')
- gain_mlp: bfloat16 [1, 4096], replicated
- w_gate: bfloat16 [1, 4096, 11008], P(None, None, 'model')
- w_up: bfloat16 [1, 4096, 11008], P(None, None, 'model')
- w_down: bfloat16 [1, 11008, 4096], P(None, 'model')
- gain_final: bfloat16 [4096], replicated
- w_vocab: bfloat16 [4096, 32000], P(None, 'model')
Outputs:
- output 1: bfloat16 [1, 32, 512, 32, 128], P(None, ('data', 'beam'), None, 'model')
- output 2: bfloat16 [1, 32, 512, 32, 128], P(None, ('data', 'beam'), None, 'model')
- output 3: float32 [32, 32000], P(('data', 'beam'), 'model')
All inputs are finite; a program needn't handle non-finite values.
Results may differ from a plain program's by a relative error of at most 0.001.
Values are sent between devices in bfloat16 or wider.
A program may use at most 768 MiB of HBM per device.

v0:
```python
import jax
import jax.numpy as jnp
from jax import lax
from jax.sharding import PartitionSpec as P

NORM_EPS = 1e-6
ROPE_BASE = 10000.0


def rms_norm(residual, gain):
    inv_rms = lax.rsqrt(jnp.mean(residual * residual, axis=-1, keepdims=True) + NORM_EPS)
    return (residual * inv_rms * gain.astype(jnp.float32)).astype(jnp.bfloat16)


def rope_rotate(vectors, position):
    half_dim = vectors.shape[-1] // 2
    inv_freq = ROPE_BASE ** (-jnp.arange(half_dim, dtype=jnp.float32) / half_dim)
    angles = position.astype(jnp.float32) * inv_freq
    cos_part = jnp.cos(angles)
    sin_part = jnp.sin(angles)
    lower_half = vectors[..., :half_dim]
    upper_half = vectors[..., half_dim:]
    return jnp.concatenate([lower_half * cos_part - upper_half * sin_part, upper_half * cos_part + lower_half * sin_part], axis=-1)


def layer_body(residual, k_sel, v_sel, position, gain_attn, w_query, w_key, w_value, w_out, gain_mlp, w_gate, w_up, w_down):
    beam_rows, cache_len, kv_local, head_dim = k_sel.shape
    heads_local = w_query.shape[1] // head_dim
    group_size = heads_local // kv_local
    normed = rms_norm(residual, gain_attn)
    q_rot = rope_rotate(jnp.dot(normed, w_query, preferred_element_type=jnp.float32).reshape(beam_rows, heads_local, head_dim), position).astype(jnp.bfloat16)
    k_new = rope_rotate(jnp.dot(normed, w_key, preferred_element_type=jnp.float32).reshape(beam_rows, kv_local, head_dim), position).astype(jnp.bfloat16)
    v_new = jnp.dot(normed, w_value, preferred_element_type=jnp.float32).astype(jnp.bfloat16).reshape(beam_rows, kv_local, head_dim)
    k_sel = lax.dynamic_update_slice(k_sel, k_new[:, None], (0, position, 0, 0))
    v_sel = lax.dynamic_update_slice(v_sel, v_new[:, None], (0, position, 0, 0))
    slot_mask = (jnp.arange(cache_len) <= position)[None, None, None, :]
    q_grouped = q_rot.reshape(beam_rows, kv_local, group_size, head_dim)
    logits = jnp.einsum('bkgd,bskd->bkgs', q_grouped, k_sel, preferred_element_type=jnp.float32) * head_dim ** -0.5
    logits = jnp.where(slot_mask, logits, -jnp.inf)
    attn_prob = jax.nn.softmax(logits, axis=-1).astype(jnp.bfloat16)
    attn_out = jnp.einsum('bkgs,bskd->bkgd', attn_prob, v_sel, preferred_element_type=jnp.float32).astype(jnp.bfloat16)
    attn_part = jnp.dot(attn_out.reshape(beam_rows, heads_local * head_dim), w_out, preferred_element_type=jnp.float32)
    residual = residual + lax.psum(attn_part, 'model')
    normed = rms_norm(residual, gain_mlp)
    gate_proj = jnp.dot(normed, w_gate, preferred_element_type=jnp.float32)
    up_proj = jnp.dot(normed, w_up, preferred_element_type=jnp.float32)
    hidden = (jax.nn.silu(gate_proj) * up_proj).astype(jnp.bfloat16)
    residual = residual + lax.psum(jnp.dot(hidden, w_down, preferred_element_type=jnp.float32), 'model')
    return residual, k_sel, v_sel


def vocab_log_softmax(logits):
    local_max = jnp.max(logits, axis=-1, keepdims=True)
    global_max = lax.pmax(local_max, 'model')
    sum_exp = lax.psum(jnp.sum(jnp.exp(logits - global_max), axis=-1, keepdims=True), 'model')
    return logits - global_max - jnp.log(sum_exp)


def solution(mesh):
    beam_size = mesh.shape['beam']
    cache_spec = P(None, ('data', 'beam'), None, 'model', None)
    col_spec = P(None, None, 'model')
    row_spec = P(None, 'model', None)
    in_specs = (P(('data', 'beam'), None), P('data', None), P(), P(('data', 'beam')), cache_spec, cache_spec,
                P(), col_spec, col_spec, col_spec, row_spec, P(), col_spec, col_spec, row_spec, P(), P(None, 'model'))
    out_specs = (cache_spec, cache_spec, P(('data', 'beam'), 'model'))

    def local_step(x_embed, parent, position, score, k_cache, v_cache, gain_attn, w_query, w_key, w_value, w_out, gain_mlp, w_gate, w_up, w_down, gain_final, w_vocab):
        layers = k_cache.shape[0]
        beam_rows = x_embed.shape[0]
        sent_span = parent.shape[1] // beam_rows
        my_index = lax.axis_index('beam')
        block_start = (my_index // sent_span) * sent_span
        my_pos = my_index - block_start
        flat_parent = parent.reshape(-1)
        my_parent = lax.dynamic_slice(flat_parent, (my_index * beam_rows,), (beam_rows,))
        src_shift = (my_pos - (my_parent // beam_rows - block_start)) % sent_span
        pick_index = src_shift * beam_rows + jnp.where(src_shift == 0, my_parent % beam_rows, jnp.arange(beam_rows, dtype=jnp.int32))
        send_index = []
        permutations = []
        for shift_by in range(1, sent_span):
            partner = block_start + (my_pos + shift_by) % sent_span
            partner_parent = lax.dynamic_slice(flat_parent, (partner * beam_rows,), (beam_rows,))
            send_index.append(jnp.clip(partner_parent - my_index * beam_rows, 0, beam_rows - 1))
            permutations.append([(device_id, (device_id // sent_span) * sent_span + (device_id % sent_span + shift_by) % sent_span) for device_id in range(beam_size)])

        def reorder(cache_layer):
            pooled = [cache_layer]
            for step_idx in range(sent_span - 1):
                outgoing = jnp.take(cache_layer, send_index[step_idx], axis=0)
                pooled.append(lax.ppermute(outgoing, 'beam', permutations[step_idx]))
            return jnp.take(jnp.concatenate(pooled, axis=0), pick_index, axis=0)

        group_score = lax.all_gather(score, 'beam', tiled=True)
        parent_score = jnp.take(group_score, my_parent)
        residual = x_embed.astype(jnp.float32)
        k_layers = []
        v_layers = []
        for layer_idx in range(layers):
            k_sel = reorder(k_cache[layer_idx])
            v_sel = reorder(v_cache[layer_idx])
            residual, k_sel, v_sel = layer_body(residual, k_sel, v_sel, position, gain_attn[layer_idx], w_query[layer_idx], w_key[layer_idx], w_value[layer_idx], w_out[layer_idx], gain_mlp[layer_idx], w_gate[layer_idx], w_up[layer_idx], w_down[layer_idx])
            k_layers.append(k_sel)
            v_layers.append(v_sel)
        logits = jnp.dot(rms_norm(residual, gain_final), w_vocab, preferred_element_type=jnp.float32)
        candidates = parent_score[:, None] + vocab_log_softmax(logits)
        return jnp.stack(k_layers), jnp.stack(v_layers), candidates

    return jax.shard_map(local_step, mesh=mesh, in_specs=in_specs, out_specs=out_specs, check_vma=False)
```

profile of v0, /device:TPU:97, one launch (start us, length us, event | category | flops | bytes accessed | tf_op | source)
XLA Modules:
  0.0 1059.2 jit_solution(6522432218696014919)
XLA Ops:
  8.5 5.3 gather_fusion.9
  13.8 5.3 gather_fusion.1
  19.1 7.7 broadcast_select_fusion.14
  29.4 5.3 gather_fusion.10
  39.9 7.6 broadcast_select_fusion.12
  59.3 7.5 broadcast_select_fusion.10
  68.4 5.3 gather_fusion.12
  73.8 5.2 gather_fusion.4
  79.0 7.5 broadcast_select_fusion.8
  97.3 7.5 broadcast_select_fusion.6
  123.1 5.3 gather_fusion.7
  128.4 7.7 broadcast_select_fusion.4
  140.7 52.6 %collective-permute-done.8 = bf16[4,512,8,128]{3,2,1,0:T(8,128)(2,1)} collective-permute-done((bf16[4,512,8,128]{3,2,1,0:T(8,128)(2,1)}, bf16[4,512,8,128]{3,2,1,0:T(8,128)(2,1)}, u32[]{:S(2)}, u32[]{:S(2)}) %collective-permute-start.8) | collective-permute-done | bytes 4194336 | tf_op jit(solution)/shard_map/ppermute | solution.py:91
  193.4 87.6 %collective-permute-done.9 = bf16[4,512,8,128]{3,2,1,0:T(8,128)(2,1)} collective-permute-done((bf16[4,512,8,128]{3,2,1,0:T(8,128)(2,1)}, bf16[4,512,8,128]{3,2,1,0:T(8,128)(2,1)}, u32[]{:S(2)}, u32[]{:S(2)}) %collective-permute-start.9) | collective-permute-done | bytes 4194336 | tf_op jit(solution)/shard_map/ppermute | solution.py:91
  280.9 33.1 %collective-permute-start = (bf16[4,512,8,128]{3,2,1,0:T(8,128)(2,1)}, bf16[4,512,8,128]{3,2,1,0:T(8,128)(2,1)}, u32[]{:S(2)}, u32[]{:S(2)}) collective-permute-start(bf16[4,512,8,128]{3,2,1,0:T(8,128)(2,1)} %get-tuple-element.42), channel_id=1, source_target_pairs={{0,1},{1,2},{2,3},{3,4},{4,5},{5,6},{6,7},{7,0},{8,9},{9,10},{10,1... | collective-permute-start | bytes 12582920 | tf_op jit(solution)/shard_map/ppermute | solution.py:91
  314.1 60.1 %collective-permute-done.10 = bf16[4,512,8,128]{3,2,1,0:T(8,128)(2,1)} collective-permute-done((bf16[4,512,8,128]{3,2,1,0:T(8,128)(2,1)}, bf16[4,512,8,128]{3,2,1,0:T(8,128)(2,1)}, u32[]{:S(2)}, u32[]{:S(2)}) %collective-permute-start.10) | collective-permute-done | bytes 4194336 | tf_op jit(solution)/shard_map/ppermute | solution.py:91
  374.9 11.4 %copy.39 = bf16[1024,4096]{1,0:T(8,128)(2,1)} copy(bf16[1024,4096]{0,1:T(8,128)(2,1)} %bitcast.147) | data formatting | bytes 16777216 | tf_op jit(solution)/shard_map/dot_general | solution.py:31
  386.2 11.6 %copy.38 = bf16[1024,4096]{1,0:T(8,128)(2,1)} copy(bf16[1024,4096]{0,1:T(8,128)(2,1)} %bitcast.148) | data formatting | bytes 16777216 | tf_op jit(solution)/shard_map/dot_general | solution.py:32
  398.0 5.8 fusion.41
  406.1 5.4 collective-permute-done.11
  411.6 36.6 %collective-permute-done.12 = bf16[4,512,8,128]{3,2,1,0:T(8,128)(2,1)} collective-permute-done((bf16[4,512,8,128]{3,2,1,0:T(8,128)(2,1)}, bf16[4,512,8,128]{3,2,1,0:T(8,128)(2,1)}, u32[]{:S(2)}, u32[]{:S(2)}) %collective-permute-start.12) | collective-permute-done | bytes 4194336 | tf_op jit(solution)/shard_map/ppermute | solution.py:91
  451.8 287.5 %all-reduce = f32[32]{0:T(128)S(1)} all-reduce(f32[32]{0:T(128)S(1)} %dynamic-update-slice), channel_id=1, replica_groups=mesh['data'=1,'model'=4,'beam'=8] {'beam'}, use_global_device_ids=true, to_apply=%add | all-reduce | flops 32 | bytes 256
  810.8 21.1 %collective-permute-done.5 = bf16[4,512,8,128]{3,2,1,0:T(8,128)(2,1)} collective-permute-done((bf16[4,512,8,128]{3,2,1,0:T(8,128)(2,1)}, bf16[4,512,8,128]{3,2,1,0:T(8,128)(2,1)}, u32[]{:S(2)}, u32[]{:S(2)}) %collective-permute-start.5) | collective-permute-done | bytes 4194336 | tf_op jit(solution)/shard_map/ppermute | solution.py:91
  836.3 40.7 %collective-permute-done.6 = bf16[4,512,8,128]{3,2,1,0:T(8,128)(2,1)} collective-permute-done((bf16[4,512,8,128]{3,2,1,0:T(8,128)(2,1)}, bf16[4,512,8,128]{3,2,1,0:T(8,128)(2,1)}, u32[]{:S(2)}, u32[]{:S(2)}) %collective-permute-start.6) | collective-permute-done | bytes 4194336 | tf_op jit(solution)/shard_map/ppermute | solution.py:91
  905.4 35.3 %all-reduce.4.cloned.1.call-done = f32[4,4096]{1,0:T(4,128)} async-done(((f32[4,4096]{1,0:T(4,128)}), f32[4,4096]{1,0:T(4,128)}) %all-reduce.4.cloned.1.call-update) | async-done | bytes 65552 | tf_op jit(solution)/shard_map/psum | solution.py:43
  942.6 10.4 fusion.6
  953.1 10.5 fusion.19
  963.6 11.1 %fusion.2 = f32[4,4096]{1,0:T(4,128)} fusion(bf16[4,2752]{1,0:T(4,128)(2,1)S(1)} %fusion.19, bf16[1,2752,4096]{2,1,0:T(8,128)(2,1)} %param.35), kind=kOutput, calls=%fused_computation.19 | convolution fusion | flops 90177536 | bytes 22631936 | tf_op jit(solution)/shard_map/dot_general | solution.py:48
  974.8 36.5 %all-reduce.6.cloned.1.call-done = f32[4,4096]{1,0:T(4,128)} async-done(((f32[4,4096]{1,0:T(4,128)}), f32[4,4096]{1,0:T(4,128)}) %all-reduce.6.cloned.1.call-update) | async-done | bytes 65552 | tf_op jit(solution)/shard_map/psum | solution.py:48
  1012.3 25.1 %fusion.81 = (f32[4]{0:T(128)S(1)}, f32[4,8000]{1,0:T(4,128)S(1)}) fusion(bf16[4096,8000]{0,1:T(8,128)(2,1)} %param.37, f32[4096]{0:T(1024)S(1)} %convert_element_type.56, f32[4]{0:T(128)S(1)} %add_rsqrt_fusion, f32[4,4096]{1,0:T(4,128)} %all-reduce.6.cloned.1.call-done, f32[4,4096]{1,0:T(4,128)S(1)} %copy-done.7, bf16[4,4096]{1,0:T(4,128)(2,1)S(1)} %copy-done.6), kind=kOutput, calls=%fused_computation.189 | convolution fusion | flops 262274304 | bytes 65844256 | tf_op jit(solution)/shard_map/dot_general | solution.py:105
  1037.4 7.4 pmax.7
  1045.0 6.1 psum.23
  (123 shorter events, 169.9 us)
Async XLA Ops:
  7.2 933.5 %all-reduce.4.cloned.1.call-start = ((), (), s32[]{:S(2)}) async-start(), calls=%async_computation | async-start | bytes 131072 | tf_op jit(solution)/shard_map/psum | solution.py:43
  26.7 109.3 %collective-permute-start.7 = (bf16[4,512,8,128]{3,2,1,0:T(8,128)(2,1)}, bf16[4,512,8,128]{3,2,1,0:T(8,128)(2,1)}, u32[]{:S(2)}, u32[]{:S(2)}) collective-permute-start(bf16[4,512,8,128]{3,2,1,0:T(8,128)(2,1)} %get-tuple-element.41), channel_id=1, source_target_pairs={{0,1},{1,2},{2,3},{3,4},{4,5},{5,6},{6,7},{7,0},{8,9},{9,10},{10,1... | collective-permute-start | bytes 12582920 | tf_op jit(solution)/shard_map/ppermute | solution.py:91
  47.5 145.9 %collective-permute-start.8 = (bf16[4,512,8,128]{3,2,1,0:T(8,128)(2,1)}, bf16[4,512,8,128]{3,2,1,0:T(8,128)(2,1)}, u32[]{:S(2)}, u32[]{:S(2)}) collective-permute-start(bf16[4,512,8,128]{3,2,1,0:T(8,128)(2,1)} %get-tuple-element.39), channel_id=1, source_target_pairs={{0,2},{1,3},{2,4},{3,5},{4,6},{5,7},{6,0},{7,1},{8,10},{9,11},{10,... | collective-permute-start | bytes 12582920 | tf_op jit(solution)/shard_map/ppermute | solution.py:91
  66.8 214.2 %collective-permute-start.9 = (bf16[4,512,8,128]{3,2,1,0:T(8,128)(2,1)}, bf16[4,512,8,128]{3,2,1,0:T(8,128)(2,1)}, u32[]{:S(2)}, u32[]{:S(2)}) collective-permute-start(bf16[4,512,8,128]{3,2,1,0:T(8,128)(2,1)} %get-tuple-element.37), channel_id=1, source_target_pairs={{0,3},{1,4},{2,5},{3,6},{4,7},{5,0},{6,1},{7,2},{8,11},{9,12},{10,... | collective-permute-start | bytes 12582920 | tf_op jit(solution)/shard_map/ppermute | solution.py:91
  86.5 287.6 %collective-permute-start.10 = (bf16[4,512,8,128]{3,2,1,0:T(8,128)(2,1)}, bf16[4,512,8,128]{3,2,1,0:T(8,128)(2,1)}, u32[]{:S(2)}, u32[]{:S(2)}) collective-permute-start(bf16[4,512,8,128]{3,2,1,0:T(8,128)(2,1)} %get-tuple-element.35), channel_id=1, source_target_pairs={{0,4},{1,5},{2,6},{3,7},{4,0},{5,1},{6,2},{7,3},{8,12},{9,13},{10,... | collective-permute-start | bytes 12582920 | tf_op jit(solution)/shard_map/ppermute | solution.py:91
  104.8 306.7 %collective-permute-start.11 = (bf16[4,512,8,128]{3,2,1,0:T(8,128)(2,1)}, bf16[4,512,8,128]{3,2,1,0:T(8,128)(2,1)}, u32[]{:S(2)}, u32[]{:S(2)}) collective-permute-start(bf16[4,512,8,128]{3,2,1,0:T(8,128)(2,1)} %get-tuple-element.33), channel_id=1, source_target_pairs={{0,5},{1,6},{2,7},{3,0},{4,1},{5,2},{6,3},{7,4},{8,13},{9,14},{10,... | collective-permute-start | bytes 12582920 | tf_op jit(solution)/shard_map/ppermute | solution.py:91
  128.4 8.1 copy-start.2
  128.4 8.1 copy-start.3
  136.0 312.1 %collective-permute-start.12 = (bf16[4,512,8,128]{3,2,1,0:T(8,128)(2,1)}, bf16[4,512,8,128]{3,2,1,0:T(8,128)(2,1)}, u32[]{:S(2)}, u32[]{:S(2)}) collective-permute-start(bf16[4,512,8,128]{3,2,1,0:T(8,128)(2,1)} %get-tuple-element.31), channel_id=1, source_target_pairs={{0,6},{1,7},{2,0},{3,1},{4,2},{5,3},{6,4},{7,5},{8,14},{9,15},{10,... | collective-permute-start | bytes 12582920 | tf_op jit(solution)/shard_map/ppermute | solution.py:91
  136.5 238.3 %copy-start.9 = (bf16[1,4096]{1,0:T(2,128)(2,1)S(1)}, bf16[1,4096]{1,0:T(2,128)(2,1)}, u32[]{:S(2)}) copy-start(bf16[1,4096]{1,0:T(2,128)(2,1)} %param.27) | copy-start | bytes 24580
  193.3 256.9 %collective-permute-start.13 = (bf16[4,512,8,128]{3,2,1,0:T(8,128)(2,1)}, bf16[4,512,8,128]{3,2,1,0:T(8,128)(2,1)}, u32[]{:S(2)}, u32[]{:S(2)}) collective-permute-start(bf16[4,512,8,128]{3,2,1,0:T(8,128)(2,1)} %get-tuple-element.29), channel_id=1, source_target_pairs={{0,7},{1,0},{2,1},{3,2},{4,3},{5,4},{6,5},{7,6},{8,15},{9,8},{10,9... | collective-permute-start | bytes 12582920 | tf_op jit(solution)/shard_map/ppermute | solution.py:91
  280.9 458.5 %collective-permute-start = (bf16[4,512,8,128]{3,2,1,0:T(8,128)(2,1)}, bf16[4,512,8,128]{3,2,1,0:T(8,128)(2,1)}, u32[]{:S(2)}, u32[]{:S(2)}) collective-permute-start(bf16[4,512,8,128]{3,2,1,0:T(8,128)(2,1)} %get-tuple-element.42), channel_id=1, source_target_pairs={{0,1},{1,2},{2,3},{3,4},{4,5},{5,6},{6,7},{7,0},{8,9},{9,10},{10,1... | collective-permute-start | bytes 12582920 | tf_op jit(solution)/shard_map/ppermute | solution.py:91
  374.2 366.5 %collective-permute-start.1 = (bf16[4,512,8,128]{3,2,1,0:T(8,128)(2,1)}, bf16[4,512,8,128]{3,2,1,0:T(8,128)(2,1)}, u32[]{:S(2)}, u32[]{:S(2)}) collective-permute-start(bf16[4,512,8,128]{3,2,1,0:T(8,128)(2,1)} %get-tuple-element.40), channel_id=1, source_target_pairs={{0,2},{1,3},{2,4},{3,5},{4,6},{5,7},{6,0},{7,1},{8,10},{9,11},{10,... | collective-permute-start | bytes 12582920 | tf_op jit(solution)/shard_map/ppermute | solution.py:91
  386.2 11.6 %copy-start.6 = (bf16[4,4096]{1,0:T(4,128)(2,1)S(1)}, bf16[4,4096]{1,0:T(4,128)(2,1)}, u32[]{:S(2)}) copy-start(bf16[4,4096]{1,0:T(4,128)(2,1)} %param.21) | copy-start | bytes 98308
  398.0 5.8 copy-start.1
  403.8 46.5 %copy-start.10 = (bf16[1,4096]{1,0:T(2,128)(2,1)S(1)}, bf16[1,4096]{1,0:T(2,128)(2,1)}, u32[]{:S(2)}) copy-start(bf16[1,4096]{1,0:T(2,128)(2,1)} %param.32) | copy-start | bytes 24580
  403.8 46.5 %copy-start.13 = (u32[32]{0:T(128)S(1)}, u32[32]{0:T(128)}, u32[]{:S(2)}) copy-start(u32[32]{0:T(128)} %constant.168) | copy-start | bytes 388
  403.8 47.7 %copy-start.12 = (f32[4]{0:T(128)S(1)}, f32[4]{0:T(128)}, u32[]{:S(2)}) copy-start(f32[4]{0:T(128)} %param.24) | copy-start | bytes 52
  403.8 336.7 %copy-start.8 = (s32[1,32]{1,0:T(1,128)S(1)}, s32[1,32]{1,0:T(1,128)}, u32[]{:S(2)}) copy-start(s32[1,32]{1,0:T(1,128)} %param.22) | copy-start | bytes 388
  411.5 386.0 %collective-permute-start.2 = (bf16[4,512,8,128]{3,2,1,0:T(8,128)(2,1)}, bf16[4,512,8,128]{3,2,1,0:T(8,128)(2,1)}, u32[]{:S(2)}, u32[]{:S(2)}) collective-permute-start(bf16[4,512,8,128]{3,2,1,0:T(8,128)(2,1)} %get-tuple-element.38), channel_id=1, source_target_pairs={{0,3},{1,4},{2,5},{3,6},{4,7},{5,0},{6,1},{7,2},{8,11},{9,12},{10,... | collective-permute-start | bytes 12582920 | tf_op jit(solution)/shard_map/ppermute | solution.py:91
  448.2 353.8 %collective-permute-start.3 = (bf16[4,512,8,128]{3,2,1,0:T(8,128)(2,1)}, bf16[4,512,8,128]{3,2,1,0:T(8,128)(2,1)}, u32[]{:S(2)}, u32[]{:S(2)}) collective-permute-start(bf16[4,512,8,128]{3,2,1,0:T(8,128)(2,1)} %get-tuple-element.36), channel_id=1, source_target_pairs={{0,4},{1,5},{2,6},{3,7},{4,0},{5,1},{6,2},{7,3},{8,12},{9,13},{10,... | collective-permute-start | bytes 12582920 | tf_op jit(solution)/shard_map/ppermute | solution.py:91
  450.3 356.1 %collective-permute-start.4 = (bf16[4,512,8,128]{3,2,1,0:T(8,128)(2,1)}, bf16[4,512,8,128]{3,2,1,0:T(8,128)(2,1)}, u32[]{:S(2)}, u32[]{:S(2)}) collective-permute-start(bf16[4,512,8,128]{3,2,1,0:T(8,128)(2,1)} %get-tuple-element.34), channel_id=1, source_target_pairs={{0,5},{1,6},{2,7},{3,0},{4,1},{5,2},{6,3},{7,4},{8,13},{9,14},{10,... | collective-permute-start | bytes 12582920 | tf_op jit(solution)/shard_map/ppermute | solution.py:91
  739.5 92.4 %collective-permute-start.5 = (bf16[4,512,8,128]{3,2,1,0:T(8,128)(2,1)}, bf16[4,512,8,128]{3,2,1,0:T(8,128)(2,1)}, u32[]{:S(2)}, u32[]{:S(2)}) collective-permute-start(bf16[4,512,8,128]{3,2,1,0:T(8,128)(2,1)} %get-tuple-element.32), channel_id=1, source_target_pairs={{0,6},{1,7},{2,0},{3,1},{4,2},{5,3},{6,4},{7,5},{8,14},{9,15},{10,... | collective-permute-start | bytes 12582920 | tf_op jit(solution)/shard_map/ppermute | solution.py:91
  740.7 5.3 copy-start
  740.7 136.3 %collective-permute-start.6 = (bf16[4,512,8,128]{3,2,1,0:T(8,128)(2,1)}, bf16[4,512,8,128]{3,2,1,0:T(8,128)(2,1)}, u32[]{:S(2)}, u32[]{:S(2)}) collective-permute-start(bf16[4,512,8,128]{3,2,1,0:T(8,128)(2,1)} %get-tuple-element.30), channel_id=1, source_target_pairs={{0,7},{1,0},{2,1},{3,2},{4,3},{5,4},{6,5},{7,6},{8,15},{9,8},{10,9... | collective-permute-start | bytes 12582920 | tf_op jit(solution)/shard_map/ppermute | solution.py:91
  890.7 2.0 copy-start.5
  892.7 2.0 copy-start.4
  904.4 106.9 %all-reduce.6.cloned.1.call-start = ((), (), s32[]{:S(2)}) async-start(), calls=%async_computation.1 | async-start | bytes 131072 | tf_op jit(solution)/shard_map/psum | solution.py:48
  963.5 11.3 %copy-start.11 = (bf16[4096]{0:T(1024)(128)(2,1)S(1)}, bf16[4096]{0:T(1024)(128)(2,1)}, u32[]{:S(2)}) copy-start(bf16[4096]{0:T(1024)(128)(2,1)} %param.36) | copy-start | bytes 24580
  963.6 47.7 %copy-start.7 = (f32[4,4096]{1,0:T(4,128)S(1)}, f32[4,4096]{1,0:T(4,128)}, u32[]{:S(2)}) copy-start(f32[4,4096]{1,0:T(4,128)} %all-reduce.4.cloned.1.call-done) | copy-start | bytes 196612
Sparse Core Ops, SparseCore 0:
  904.5 36.1 all-reduce.3
  974.8 36.4 all-reduce.5
where the time goes:
time: 1070 us; the launch traced here: 1060 us
  waiting for transfers between devices  376 us (35%)
  blocking collectives  301 us (28%)
  local copies, waits for them, and re-layouts  181 us (17%)
  matrix products  79.1 us (7%)
  other arithmetic  59.8 us (6%)
  starting transfers between devices  45.9 us (4%)
  between operations  16.3 us (2%)
    ppermute x14, waiting for transfers between devices, reorder(): pooled.append(lax.ppermute(outgoing, 'beam', permutations[step_idx]))  304 us
    unnamed x1, blocking collectives  288 us
    gather x14, local copies, waits for them, and re-layouts, reorder(): outgoing = jnp.take(cache_layer, send_index[step_idx], axis=0)  73.5 us
    unnamed x45, local copies, waits for them, and re-layouts  64.9 us
    select_n x7, other arithmetic, reorder(): outgoing = jnp.take(cache_layer, send_index[step_idx], axis=0)  49.6 us
    ppermute x14, starting transfers between devices, reorder(): pooled.append(lax.ppermute(outgoing, 'beam', permutations[step_idx]))  45.5 us
    psum x1, waiting for transfers between devices, layer_body(): lax.psum(jnp.dot(hidden, w_down, preferred_element_type=jnp.float32), 'mo...  36.5 us
    psum x1, waiting for transfers between devices, layer_body(): residual = residual + lax.psum(attn_part, 'model')  35.3 us
  transfers between devices with their start and end apart: 16, of which 10 were waited for; matrix products, arithmetic and copies ran while one was open for 20% of the time, Pallas kernels for 0%

commit v1 on v0

v1 whole, which is shorter than its diff:
```python
import functools

import jax
import jax.numpy as jnp
from jax import lax
from jax.experimental import pallas as pl
from jax.experimental.pallas import tpu as pltpu
from jax.sharding import PartitionSpec as P

NORM_EPS = 1e-6
ROPE_BASE = 10000.0
MESH = pl.DeviceIdType.MESH
CHUNKS = 4
TABLE = 24
ROUND_CHOICES = (3, 4)


def rms_norm(residual, gain):
    inv_rms = lax.rsqrt(jnp.mean(residual * residual, axis=-1, keepdims=True) + NORM_EPS)
    return (residual * inv_rms * gain.astype(jnp.float32)).astype(jnp.bfloat16)


def rope_rotate(vectors, position):
    half_dim = vectors.shape[-1] // 2
    inv_freq = ROPE_BASE ** (-jnp.arange(half_dim, dtype=jnp.float32) / half_dim)
    angles = position.astype(jnp.float32) * inv_freq
    cos_part = jnp.cos(angles)
    sin_part = jnp.sin(angles)
    lower_half = vectors[..., :half_dim]
    upper_half = vectors[..., half_dim:]
    return jnp.concatenate([lower_half * cos_part - upper_half * sin_part, upper_half * cos_part + lower_half * sin_part], axis=-1)


def plan_kernel(chips, chip_rows, parent_ref, table_ref, info_ref, need, via, hop1, hop2, load, own, two):
    total = chips * chip_rows
    my_chip = lax.axis_index("beam") // 2

    def each(n, body):
        lax.fori_loop(0, n, lambda i, _: (body(i), 0)[1], 0)

    def clear_rows(q):
        need[q] = 0
        via[q] = 0
        hop1[q] = 0
        hop1[total + q] = 0
        hop2[q] = 0

    def clear_links(i):
        load[i] = 0
        own[i] = 0
        two[i] = 0

    def clear_table(i):
        table_ref[i] = 0

    each(total, clear_rows)
    each(2 * chips, clear_links)
    each(2 * TABLE + chip_rows, clear_table)

    def mark(b):
        q = parent_ref[0, b]
        dist = lax.rem(b // chip_rows - q // chip_rows + chips, chips)
        need[q] = need[q] | (1 << dist)

    each(total, mark)

    def bits(q):
        n = need[q]
        return (n >> 1) & 1, (n >> 2) & 1, (n >> 3) & 1

    def up(c):
        return lax.rem(c + 1, chips)

    def down(c):
        return chips + lax.rem(c + chips - 1, chips)

    def fixed(q):
        c = q // chip_rows
        a, b, d = bits(q)
        plus = b * a * (1 - d)
        minus = b * d * (1 - a)
        own[c] = own[c] + a
        own[chips + c] = own[chips + c] + d
        load[c] = load[c] + a
        load[chips + c] = load[chips + c] + d
        load[up(c)] = load[up(c)] + plus
        load[down(c)] = load[down(c)] + minus
        via[q] = plus + 2 * minus

    each(total, fixed)

    def free(q):
        c = q // chip_rows
        a, b, d = bits(q)
        flex = b * (1 - (a ^ d))
        cost_plus = jnp.maximum(load[c] + 1 - a, load[up(c)] + 1)
        cost_minus = jnp.maximum(load[chips + c] + 1 - d, load[down(c)] + 1)
        side = (cost_plus <= cost_minus).astype(jnp.int32)
        plus = flex * side
        minus = flex * (1 - side)
        load[c] = load[c] + plus * (1 - a)
        own[c] = own[c] + plus * (1 - a)
        load[chips + c] = load[chips + c] + minus * (1 - d)
        own[chips + c] = own[chips + c] + minus * (1 - d)
        load[up(c)] = load[up(c)] + plus
        load[down(c)] = load[down(c)] + minus
        via[q] = via[q] + plus + 2 * minus

    each(total, free)

    def first_two(q):
        c = q // chip_rows
        v = via[q]
        plus = v & 1
        minus = v >> 1
        hop1[q] = two[c] * plus
        hop1[total + q] = two[chips + c] * minus
        two[c] = two[c] + plus
        two[chips + c] = two[chips + c] + minus

    each(total, first_two)

    def restart(i):
        load[i] = two[i]

    each(2 * chips, restart)

    def rest(q, rounds):
        c = q // chip_rows
        a, b, d = bits(q)
        v = via[q]
        plus = v & 1
        minus = v >> 1
        a1 = a * (1 - plus)
        d1 = d * (1 - minus)
        hop1[q] = hop1[q] + a1 * load[c]
        hop1[total + q] = hop1[total + q] + d1 * load[chips + c]
        load[c] = load[c] + a1
        load[chips + c] = load[chips + c] + d1
        onward = plus * (jnp.maximum(own[up(c)], 1) + hop1[q]) + minus * (jnp.maximum(own[down(c)], 1) + hop1[total + q])
        hop2[q] = onward
        used = jnp.maximum(onward + 1, jnp.maximum((hop1[q] + 1) * (a | plus), (hop1[total + q] + 1) * (d | minus)))
        return jnp.maximum(rounds, used * jnp.minimum(need[q] >> 1, 1))

    info_ref[0] = lax.fori_loop(0, total, rest, 0)

    def fill(q):
        c = q // chip_rows
        a, b, d = bits(q)
        v = via[q]

        @pl.when((c == my_chip) & ((a | (v & 1)) == 1))
        def _():
            table_ref[hop1[q]] = lax.rem(q, chip_rows)

        @pl.when((c == my_chip) & ((d | (v >> 1)) == 1))
        def _():
            table_ref[TABLE + hop1[total + q]] = lax.rem(q, chip_rows)

        @pl.when((up(c) == my_chip) & ((v & 1) == 1))
        def _():
            table_ref[hop2[q]] = chip_rows + hop1[q]

        @pl.when((down(c) == chips + my_chip) & ((v >> 1) == 1))
        def _():
            table_ref[TABLE + hop2[q]] = chip_rows + hop1[total + q]

    each(total, fill)

    def place(j):
        q = parent_ref[0, my_chip * chip_rows + j]
        dist = lax.rem(my_chip - q // chip_rows + chips, chips)
        v = via[q]
        at_plus = chip_rows + 2 * jnp.where(dist == 1, hop1[q], hop2[q])
        at_minus = chip_rows + 2 * jnp.where(dist == 3, hop1[total + q], hop2[q]) + 1
        from_plus = (dist == 1) | ((dist == 2) & ((v & 1) == 1))
        where = jnp.where(from_plus, at_plus, at_minus)
        table_ref[2 * TABLE + j] = jnp.where(dist == 0, lax.rem(q, chip_rows), where)

    each(chip_rows, place)


def make_plan(parent, chips, chip_rows):
    total = chips * chip_rows
    smem = pl.BlockSpec(memory_space=pltpu.SMEM)
    return pl.pallas_call(
        functools.partial(plan_kernel, chips, chip_rows),
        out_shape=(jax.ShapeDtypeStruct((2 * TABLE + chip_rows,), jnp.int32), jax.ShapeDtypeStruct((1,), jnp.int32)),
        in_specs=[smem],
        out_specs=(smem, smem),
        scratch_shapes=[
            pltpu.SMEM((total,), jnp.int32),
            pltpu.SMEM((total,), jnp.int32),
            pltpu.SMEM((2 * total,), jnp.int32),
            pltpu.SMEM((total,), jnp.int32),
            pltpu.SMEM((2 * chips,), jnp.int32),
            pltpu.SMEM((2 * chips,), jnp.int32),
            pltpu.SMEM((2 * chips,), jnp.int32),
        ],
        name="plan",
    )(parent)


def move_kernel(rounds, beams, rows, block, table, k_ref, v_ref, k_out, v_out, *scratch):
    nchunk = CHUNKS
    pool = scratch[:nchunk]
    recv = scratch[nchunk : 2 * nchunk]
    send = scratch[2 * nchunk : 3 * nchunk]
    stage = scratch[3 * nchunk : 4 * nchunk]
    pool_sem, swap_send, swap_recv, send_sem, recv_sem, out_sem, give_send, give_recv = scratch[4 * nchunk :]
    me = lax.axis_index("beam")
    core = lax.rem(me, 2)
    sibling = me + 1 - 2 * core
    right = lax.rem(me + 2, beams)
    left = lax.rem(me + beams - 2, beams)
    mine = pl.ds(core * rows, rows)
    theirs = pl.ds((1 - core) * rows, rows)
    chip_rows = 2 * rows

    def part(ref, c):
        return ref.at[:, pl.ds(c * block, block), :]

    def load_own(ref, c):
        return pltpu.make_async_copy(part(ref, c), pool[c].at[mine], pool_sem.at[c])

    def swap(ref, c):
        return pltpu.make_async_remote_copy(part(ref, c), pool[c].at[mine], swap_send.at[c], swap_recv.at[c], device_id={"beam": sibling}, device_id_type=MESH)

    def hop(r, d, c):
        return pltpu.make_async_remote_copy(
            send[c].at[2 * r + d], recv[c].at[2 * r + d], send_sem.at[r, d, c], recv_sem.at[r, d, c],
            device_id={"beam": right if d == 0 else left}, device_id_type=MESH)

    def store_own(ref, c):
        return pltpu.make_async_copy(stage[c].at[mine], part(ref, c), out_sem.at[c])

    def give(ref, c):
        return pltpu.make_async_remote_copy(stage[c].at[theirs], part(ref, c), give_send.at[c], give_recv.at[c], device_id={"beam": sibling}, device_id_type=MESH)

    barrier = pltpu.get_barrier_semaphore()
    for peer in (sibling, left, right):
        pl.semaphore_signal(barrier, inc=1, device_id={"beam": peer}, device_id_type=MESH)

    @pl.when(core == 0)
    def _():
        for c in range(nchunk):
            load_own(k_ref, c).start()

    @pl.when(core == 1)
    def _():
        for c in range(nchunk):
            load_own(v_ref, c).start()

    pl.semaphore_wait(barrier, 3)

    @pl.when(core == 0)
    def _():
        for c in range(nchunk):
            swap(v_ref, c).start()

    @pl.when(core == 1)
    def _():
        for c in range(nchunk):
            swap(k_ref, c).start()

    strip = min(block, 128)

    def build(r, c):
        for d in (0, 1):
            code = table[d * TABLE + r]
            row = jnp.minimum(code, chip_rows - 1)

            def body(i, _):
                at = pl.ds(pl.multiple_of(i * strip, strip), strip)
                x = pool[c][row, at, :]
                for e in range(r):
                    x = jnp.where(code == chip_rows + e, recv[c][2 * e + d, at, :], x)
                send[c][2 * r + d, at, :] = x
                return 0

            lax.fori_loop(0, block // strip, body, 0)
        for d in (0, 1):
            hop(r, d, c).start()

    for c in range(nchunk):
        load_own(k_ref, c).wait()
        swap(k_ref, c).wait_recv()
        build(0, c)
    for r in range(1, rounds):
        for c in range(nchunk):
            for d in (0, 1):
                hop(r - 1, d, c).wait_recv()
            build(r, c)
    for c in range(nchunk):
        for d in (0, 1):
            hop(rounds - 1, d, c).wait_recv()
        for j in range(chip_rows):
            where = table[2 * TABLE + j]
            row = jnp.minimum(where, chip_rows - 1)
            slot = jnp.maximum(where - chip_rows, 0)

            def body(i, _):
                at = pl.ds(pl.multiple_of(i * strip, strip), strip)
                stage[c][j, at, :] = jnp.where(where < chip_rows, pool[c][row, at, :], recv[c][slot, at, :])
                return 0

            lax.fori_loop(0, block // strip, body, 0)

        @pl.when(core == 0)
        def _():
            give(k_out, c).start()
            store_own(k_out, c).start()

        @pl.when(core == 1)
        def _():
            give(v_out, c).start()
            store_own(v_out, c).start()

    for c in range(nchunk):
        swap(k_ref, c).wait_send()
        for r in range(rounds):
            for d in (0, 1):
                hop(r, d, c).wait_send()
        store_own(k_out, c).wait()
        give(k_out, c).wait()


def move_rows(rounds, beams, table, k_rows, v_rows):
    rows, length, lanes = k_rows.shape
    block = length // CHUNKS
    vmem = pltpu.VMEM
    hbm = pl.BlockSpec(memory_space=pl.ANY)
    dtype = k_rows.dtype
    scratch = [vmem((2 * rows, block, lanes), dtype)] * CHUNKS
    scratch += [vmem((2 * rounds, block, lanes), dtype)] * CHUNKS
    scratch += [vmem((2 * rounds, block, lanes), dtype)] * CHUNKS
    scratch += [vmem((2 * rows, block, lanes), dtype)] * CHUNKS
    sem = pltpu.SemaphoreType.DMA
    scratch += [sem((CHUNKS,)), sem((CHUNKS,)), sem((CHUNKS,)), sem((rounds, 2, CHUNKS)), sem((rounds, 2, CHUNKS)), sem((CHUNKS,)), sem((CHUNKS,)), sem((CHUNKS,))]
    out = jax.ShapeDtypeStruct(k_rows.shape, dtype)
    return pl.pallas_call(
        functools.partial(move_kernel, rounds, beams, rows, block),
        out_shape=(out, out),
        in_specs=[pl.BlockSpec(memory_space=pltpu.SMEM), hbm, hbm],
        out_specs=(hbm, hbm),
        scratch_shapes=scratch,
        compiler_params=pltpu.CompilerParams(collective_id=rounds, has_side_effects=True, vmem_limit_bytes=60 * 2**20),
        name=f"move{rounds}",
    )(table, k_rows, v_rows)


def move_any(beams, parent, k_rows, v_rows):
    rows = k_rows.shape[0]
    me = lax.axis_index("beam")
    mine = lax.dynamic_slice(parent.reshape(-1), (me * rows,), (rows,))
    ring = [(i, (i + 1) % beams) for i in range(beams)]

    def step(s, carry):
        k_here, v_here, k_sel, v_sel = carry
        source = lax.rem(me - s + beams, beams)
        hit = (mine // rows == source)[:, None, None]
        local = lax.rem(mine, rows)
        k_sel = jnp.where(hit, jnp.take(k_here, local, axis=0), k_sel)
        v_sel = jnp.where(hit, jnp.take(v_here, local, axis=0), v_sel)
        return lax.ppermute(k_here, "beam", ring), lax.ppermute(v_here, "beam", ring), k_sel, v_sel

    carry = lax.fori_loop(0, beams, step, (k_rows, v_rows, k_rows, v_rows))
    return carry[2], carry[3]


def share_kernel(axis, n, combine, x_ref, out_ref, got, send_sem, recv_sem):
    me = lax.axis_index(axis)
    barrier = pltpu.get_barrier_semaphore()
    peers = [lax.rem(me + s, n) for s in range(1, n)]
    for peer in peers:
        pl.semaphore_signal(barrier, inc=1, device_id={axis: peer}, device_id_type=MESH)
    pl.semaphore_wait(barrier, n - 1)
    copies = []
    for s, peer in enumerate(peers):
        copies.append(pltpu.make_async_remote_copy(x_ref, got.at[s], send_sem.at[s], recv_sem.at[s], device_id={axis: peer}, device_id_type=MESH))
        copies[-1].start()
    for copy in copies:
        copy.wait()
    combine(n, me, x_ref, got, out_ref)


def add_all(n, me, x_ref, got, out_ref):
    total = x_ref[...]
    for s in range(n - 1):
        total = total + got[s]
    out_ref[...] = total


def keep_all(n, me, x_ref, got, out_ref):
    out_ref[0] = x_ref[...]
    for s in range(n - 1):
        out_ref[s + 1] = got[s]


def share(x, axis, n, combine, out_shape, collective_id):
    spec = pl.BlockSpec(memory_space=pltpu.VMEM)
    return pl.pallas_call(
        functools.partial(share_kernel, axis, n, combine),
        out_shape=jax.ShapeDtypeStruct(out_shape, x.dtype),
        in_specs=[spec],
        out_specs=spec,
        scratch_shapes=[pltpu.VMEM((n - 1,) + x.shape, x.dtype), pltpu.SemaphoreType.DMA((n - 1,)), pltpu.SemaphoreType.DMA((n - 1,))],
        compiler_params=pltpu.CompilerParams(collective_id=collective_id, has_side_effects=True),
        name=f"share{collective_id}",
    )(x)


def solution(mesh):
    beams = mesh.shape["beam"]
    models = mesh.shape["model"]
    cache_spec = P(None, ('data', 'beam'), None, 'model', None)
    col_spec = P(None, None, 'model')
    row_spec = P(None, 'model', None)
    in_specs = (P(('data', 'beam'), None), P('data', None), P(), P(('data', 'beam')), cache_spec, cache_spec,
                P(), col_spec, col_spec, col_spec, row_spec, P(), col_spec, col_spec, row_spec, P(), P(None, 'model'))
    out_specs = (cache_spec, cache_spec, P(('data', 'beam'), 'model'))

    def model_sum(x, collective_id):
        if models == 1:
            return x
        return share(x, "model", models, add_all, x.shape, collective_id)

    def local_step(x_embed, parent, position, score, k_cache, v_cache, gain_attn, w_query, w_key, w_value, w_out, gain_mlp, w_gate, w_up, w_down, gain_final, w_vocab):
        rows = x_embed.shape[0]
        _, _, cache_len, heads, head_dim = k_cache.shape
        me = lax.axis_index('beam')
        table, info = make_plan(parent, beams // 2, 2 * rows)
        k_rows = k_cache.reshape(rows, cache_len * heads, head_dim)
        v_rows = v_cache.reshape(rows, cache_len * heads, head_dim)
        branch = jnp.minimum(jnp.maximum(info[0] - ROUND_CHOICES[0], 0), len(ROUND_CHOICES))
        moves = [functools.partial(move_rows, n, beams) for n in ROUND_CHOICES]
        branches = [lambda t, p, k, v, f=f: f(t, k, v) for f in moves] + [lambda t, p, k, v: move_any(beams, p, k, v)]
        k_sel, v_sel = lax.switch(branch, branches, table, parent, k_rows, v_rows)
        k_sel = k_sel.reshape(rows, cache_len, heads, head_dim)
        v_sel = v_sel.reshape(rows, cache_len, heads, head_dim)

        scores = share(jnp.broadcast_to(score[:, None], (rows, 128)), "beam", beams, keep_all, (beams, rows, 128), 10)
        mine = lax.dynamic_slice(parent.reshape(-1), (me * rows,), (rows,))
        slot = lax.rem(me - mine // rows + beams, beams)
        parent_score = scores[slot, lax.rem(mine, rows), 0]

        residual = x_embed.astype(jnp.float32)
        normed = rms_norm(residual, gain_attn[0])
        q_rot = rope_rotate(jnp.dot(normed, w_query[0], preferred_element_type=jnp.float32).reshape(rows, heads, head_dim), position).astype(jnp.bfloat16)
        k_new = rope_rotate(jnp.dot(normed, w_key[0], preferred_element_type=jnp.float32).reshape(rows, heads, head_dim), position).astype(jnp.bfloat16)
        v_new = jnp.dot(normed, w_value[0], preferred_element_type=jnp.float32).astype(jnp.bfloat16).reshape(rows, heads, head_dim)
        here = (jnp.arange(cache_len) == position)[None, :, None, None]
        k_sel = jnp.where(here, k_new[:, None], k_sel)
        v_sel = jnp.where(here, v_new[:, None], v_sel)
        slot_mask = (jnp.arange(cache_len) <= position)[None, None, :]
        logits = jnp.einsum('bkd,bskd->bks', q_rot, k_sel, preferred_element_type=jnp.float32) * head_dim ** -0.5
        logits = jnp.where(slot_mask, logits, -jnp.inf)
        attn_prob = jax.nn.softmax(logits, axis=-1).astype(jnp.bfloat16)
        attn_out = jnp.einsum('bks,bskd->bkd', attn_prob, v_sel, preferred_element_type=jnp.float32).astype(jnp.bfloat16)
        attn_part = jnp.dot(attn_out.reshape(rows, heads * head_dim), w_out[0], preferred_element_type=jnp.float32)
        residual = residual + model_sum(attn_part, 11)
        normed = rms_norm(residual, gain_mlp[0])
        gate_proj = jnp.dot(normed, w_gate[0], preferred_element_type=jnp.float32)
        up_proj = jnp.dot(normed, w_up[0], preferred_element_type=jnp.float32)
        hidden = (jax.nn.silu(gate_proj) * up_proj).astype(jnp.bfloat16)
        residual = residual + model_sum(jnp.dot(hidden, w_down[0], preferred_element_type=jnp.float32), 12)
        logits = jnp.dot(rms_norm(residual, gain_final), w_vocab, preferred_element_type=jnp.float32)
        top = jnp.max(logits, axis=-1, keepdims=True)
        mass = jnp.sum(jnp.exp(logits - top), axis=-1, keepdims=True)
        if models > 1:
            stats = jnp.concatenate([jnp.broadcast_to(top, (rows, 128)), jnp.broadcast_to(mass, (rows, 128))], axis=0)
            stats = share(stats, "model", models, keep_all, (models,) + stats.shape, 13)
            tops = stats[:, :rows, :1]
            masses = stats[:, rows:, :1]
            top = jnp.max(tops, axis=0)
            mass = jnp.sum(masses * jnp.exp(tops - top), axis=0)
        candidates = parent_score[:, None] + (logits - top - jnp.log(mass))
        return k_sel[None], v_sel[None], candidates

    return jax.shard_map(local_step, mesh=mesh, in_specs=in_specs, out_specs=out_specs, check_vma=False)
```

time: 1070 us -> 272 us (0.25)
  waiting for transfers between devices: 376 us -> 0 us
  blocking collectives: 301 us -> 0 us
  local copies, waits for them, and re-layouts: 181 us -> 47.3 us
  Pallas kernels: 0 us -> 120 us
  starting transfers between devices: 45.9 us -> 0 us
  other arithmetic: 59.8 us -> 18.7 us
  between operations: 16.3 us -> 2.16 us
    ppermute x14 -> x0, waiting for transfers between devices: 304 us -> none  [reorder(): pooled.append(lax.ppermute(outgoing, 'beam', permutations[step_idx]))]
    unnamed x1 -> x0, blocking collectives: 288 us -> none
    pallas_call x0 -> x6, Pallas kernels: none -> 120 us  [the longest x1 80.6 us: move_rows(): pl.pallas_call(functools.partial(move_kernel, rounds, beams, rows, block)...]
    gather x17 -> x1, local copies, waits for them, and re-layouts: 84.1 us -> 1.37 us  [local_step(): parent_score = scores[slot, lax.rem(mine, rows), 0]]
    psum x2 -> x0, waiting for transfers between devices: 71.8 us -> none  [the longest x1 36.5 us: layer_body(): lax.psum(jnp.dot(hidden, w_down, preferred_element_type=jnp.float32), 'mo...]
    unnamed x45 -> x19, local copies, waits for them, and re-layouts: 64.9 us -> 6.57 us
    ppermute x14 -> x0, starting transfers between devices: 45.5 us -> none  [reorder(): pooled.append(lax.ppermute(outgoing, 'beam', permutations[step_idx]))]
    select_n x10 -> x2, other arithmetic: 54 us -> 12.1 us  [the longest x1 6.43 us: local_step(): v_sel = jnp.where(here, v_new[:, None], v_sel)]
  transfers between devices with their start and end apart: 16 -> 0, of which waited for: 10 -> 0; matrix products, arithmetic and copies ran while one was open for 20% -> 0% of each run, Pallas kernels for 0% -> 0%
where the time goes in v1:
time: 272 us; the launch traced here: 271 us
  Pallas kernels  120 us (44%)
  matrix products  82.5 us (30%)
  local copies, waits for them, and re-layouts  47.3 us (17%)
  other arithmetic  18.7 us (7%)
    pallas_call x1, Pallas kernels, move_rows(): pl.pallas_call(functools.partial(move_kernel, rounds, beams, rows, block)...  80.6 us
    pallas_call x4, Pallas kernels, share(): pl.pallas_call(functools.partial(share_kernel, axis, n, combine), out_sha...  32.4 us
    dot_general x1, matrix products, local_step(): jnp.dot(rms_norm(residual, gain_final), w_vocab, preferred_element_type=j...  25.1 us
    cond x6, local copies, waits for them, and re-layouts  15.4 us
    dot_general x1, local copies, waits for them, and re-layouts, local_step(): jnp.dot(normed, w_query[0], preferred_element_type=jnp.float32)  11.4 us
    dot_general x1, local copies, waits for them, and re-layouts, local_step(): jnp.dot(normed, w_key[0], preferred_element_type=jnp.float32)  11.2 us
    dot_general x1, matrix products, local_step(): jnp.dot(hidden, w_down[0], preferred_element_type=jnp.float32)  11.1 us
    dot_general x1, matrix products, local_step(): up_proj = jnp.dot(normed, w_up[0], preferred_element_type=jnp.float32)  10.6 us

profile of v1, /device:TPU:97, one launch (start us, length us, event | category | flops | bytes accessed | tf_op | source)
XLA Modules:
  0.0 270.9 jit_solution(5974863164320289930)
XLA Ops:
  0.6 4.6 %copy.110 = bf16[1,4,512,8,128]{4,3,2,1,0:T(8,128)(2,1)} copy(bf16[1,4,512,8,128]{4,3,2,1,0:T(8,128)(2,1)} %param.28) | data formatting | bytes 8388608
  5.2 2.0 copy.111
  7.2 7.2 %plan.1 = (s32[56]{0:T(128)S(1)}, s32[1]{0:T(128)}) custom-call(s32[1,32]{1,0:T(1,128)S(1)} %copy-done.9), custom_call_target="tpu_custom_call" | custom-call | tf_op jit(solution)/shard_map/plan/pallas_call | solution.py:186
  15.0 96.0 %conditional.1 = (bf16[4,4096,128]{2,1,0:T(8,128)(2,1)}, bf16[4,4096,128]{2,1,0:T(8,128)(2,1)}, bf16[1,4,512,8,128]{4,3,2,1,0:T(8,128)(2,1)}, bf16[4,512,8,128]{...) conditional(s32[]{:T(128)} %bitcast.22, (s32[56]{0:T(128)S(1)}, ...), branch_computations={%region_1.0_spmd, %region_2.3_spmd, %region_3.7_spmd} | conditional | flops 8389756 | bytes 159388464 | solution.py:438
  15.1 80.6 %move3.1 = (bf16[4,4096,128]{2,1,0:T(8,128)(2,1)}, bf16[4,4096,128]{2,1,0:T(8,128)(2,1)}) custom-call(s32[56]{0:T(128)S(1)} %get-tuple-element.248.table, bf16[4,4096,128]{2,1,0:T(8,128)(2,1)} %get-tuple-element.249.k_ref, bf16[4,4096,128]{2,1,0:T(8,128)(2,1)} %get-tuple-element.250.v_ref), custom_call_target="tpu_custom_call" | custom-call | tf_op jit(solution)/shard_map/cond/branch_0_fun/move3/pallas_call | solution.py:341
  95.6 4.5 %copy.95 = bf16[1,4,512,8,128]{4,3,2,1,0:T(8,128)(2,1)} copy(bf16[1,4,512,8,128]{4,3,2,1,0:T(8,128)(2,1)} %bitcast.119) | data formatting | bytes 8388608 | tf_op jit(solution)/shard_map/cond
  100.1 4.6 %copy.96 = bf16[1,4,512,8,128]{4,3,2,1,0:T(8,128)(2,1)} copy(bf16[1,4,512,8,128]{4,3,2,1,0:T(8,128)(2,1)} %bitcast.2) | data formatting | bytes 8388608 | tf_op jit(solution)/shard_map/cond
  104.7 1.9 copy.104
  106.7 4.4 %copy.105 = bf16[4,512,8,128]{3,2,1,0:T(8,128)(2,1)} copy(bf16[4,512,8,128]{3,2,1,0:T(8,128)(2,1)} %bitcast.3) | data formatting | bytes 8388608 | tf_op jit(solution)/shard_map/cond
  111.9 4.6 %fusion.33 = bf16[1,4,8,128]{3,1,2,0:T(4,128)(2,1)S(1)} fusion(bf16[1,4096,1024]{2,1,0:T(8,128)(2,1)} %param.33, bf16[4,4096]{1,0:T(4,128)(2,1)S(1)} %copy-done.4, f32[4096]{0:T(1024)S(1)} %bitcast.129, f32[4]{0:T(128)S(1)} %add_rsqrt_fusion.2), kind=kOutput, calls=%fused_computation.49 | convolution fusion | flops 33624064 | bytes 8445968 | tf_op jit(solution)/shard_map/dot_general | solution.py:451
  116.6 11.4 %copy.39 = bf16[1024,4096]{1,0:T(8,128)(2,1)} copy(bf16[1024,4096]{0,1:T(8,128)(2,1)} %bitcast.127) | data formatting | bytes 16777216 | tf_op jit(solution)/shard_map/dot_general | solution.py:449
  128.0 5.6 %fusion.44 = f32[4,8,128]{2,0,1:T(4,128)S(1)} fusion(bf16[8,128,4096]{2,1,0:T(8,128)(2,1)} %bitcast.126, bf16[4,4096]{1,0:T(4,128)(2,1)S(1)} %copy-done.4, f32[4096]{0:T(1024)S(1)} %bitcast.130, f32[4]{0:T(128)S(1)} %add_rsqrt_fusion.2), kind=kOutput, calls=%fused_computation.68 | convolution fusion | flops 33619968 | bytes 8454160 | tf_op jit(solution)/shard_map/dot_general | solution.py:449
  133.7 11.2 %copy.38 = bf16[1024,4096]{1,0:T(8,128)(2,1)} copy(bf16[1024,4096]{0,1:T(8,128)(2,1)} %bitcast.128) | data formatting | bytes 16777216 | tf_op jit(solution)/shard_map/dot_general | solution.py:450
  144.9 5.6 %fusion.46 = f32[4,8,128]{2,0,1:T(4,128)S(1)} fusion(bf16[8,128,4096]{2,1,0:T(8,128)(2,1)} %bitcast.125, bf16[4,4096]{1,0:T(4,128)(2,1)S(1)} %copy-done.4, f32[4096]{0:T(1024)S(1)} %bitcast.131, f32[4]{0:T(128)S(1)} %add_rsqrt_fusion.2), kind=kOutput, calls=%fused_computation.70 | convolution fusion | flops 33619968 | bytes 8454160 | tf_op jit(solution)/shard_map/dot_general | solution.py:450
  150.8 6.4 %broadcast_select_fusion.2 = (bf16[1,4,512,8,128]{4,3,2,1,0:T(8,128)(2,1)}, bf16[1,4,512,8,128]{4,3,2,1,0:T(8,128)(2,1)}) fusion(bf16[1,4,512,8,128]{4,3,2,1,0:T(8,128)(2,1)} %get-tuple-element.287, pred[512]{0:T(512)(128)(4,1)S(1)} %get-tuple-element.331, bf16[4,8,128]{2,1,0:T(8,128)(2,1)S(1)} %bitcast.132, ...), kind=kLoop, calls=%fused_computation.39 | loop fusion | flops 4194304 | bytes 16794112 | tf_op jit(solution)/shard_map/jit(_where)/select_n | solution.py:454
  157.2 5.6 %broadcast_select_fusion.1 = (bf16[4,512,8,128]{3,2,1,0:T(8,128)(2,1)S(1)}, bf16[4,512,8,128]{3,2,1,0:T(8,128)(2,1)}) fusion(bf16[4,512,8,128]{3,2,1,0:T(8,128)(2,1)} %get-tuple-element.286, pred[512]{0:T(512)(128)(4,1)S(1)} %get-tuple-element.331, bf16[4,8,128]{2,1,0:T(8,128)(2,1)S(1)} %copy.29, bf16[4,512,8,128]{3,2,1,0:T(8,128)(2,1)} %get-tuple-element.288, ...), kind=kLoop, calls=%fused_computation.38 | loop fusion | flops 4194304 | bytes 16794112 | tf_op jit(solution)/shard_map/jit(_where)/select_n | solution.py:453
  162.9 1.2 fusion.17
  164.3 3.0 %fusion.15 = f32[4,8,1,128]{3,2,1,0:T(1,128)S(1)} fusion(bf16[4,512,8,128]{3,2,1,0:T(8,128)(2,1)} %get-tuple-element.325, bf16[4,8,512,1]{2,1,0,3:T(8,128)(2,1)S(1)} %fusion.29), kind=kOutput, calls=%fused_computation.33 | convolution fusion | flops 4194304 | bytes 4243456 | tf_op jit(solution)/shard_map/bks,bskd->bkd/dot_general | solution.py:459
  167.3 5.2 %fusion.11.x_ref = f32[4,4096]{1,0:T(4,128)} fusion(bf16[1,1024,4096]{2,1,0:T(8,128)(2,1)} %param.34, bf16[1,4,8,128]{3,2,1,0:T(8,128)(2,1)S(1)} %convert_bitcast_fusion), kind=kOutput, calls=%fused_computation.29 | convolution fusion | flops 33554432 | bytes 8462336 | tf_op jit(solution)/shard_map/dot_general | solution.py:460
  172.5 10.5 %share11.1 = f32[4,4096]{1,0:T(4,128)} custom-call(f32[4,4096]{1,0:T(4,128)} %fusion.11.x_ref), custom_call_target="tpu_custom_call" | custom-call | tf_op jit(solution)/shard_map/share11/pallas_call | solution.py:402
  183.0 1.0 multiply_reduce_fusion.1
  184.0 0.9 multiply_convert_fusion.1
  185.0 10.4 %fusion.9 = f32[4,2752]{1,0:T(4,128)S(1)} fusion(bf16[4,4096]{1,0:T(4,128)(2,1)S(1)} %multiply_convert_fusion.1, bf16[1,4096,2752]{1,2,0:T(8,128)(2,1)} %param.36), kind=kOutput, calls=%fused_computation.27 | convolution fusion | flops 90177536 | bytes 22621184 | tf_op jit(solution)/shard_map/dot_general | solution.py:463
  195.4 10.6 %fusion.22 = bf16[4,2752]{1,0:T(4,128)(2,1)S(1)} fusion(bf16[4,4096]{1,0:T(4,128)(2,1)S(1)} %multiply_convert_fusion.1, bf16[1,4096,2752]{1,2,0:T(8,128)(2,1)} %param.37, f32[4,2752]{1,0:T(4,128)S(1)} %fusion.9), kind=kOutput, calls=%fused_computation.42 | convolution fusion | flops 90243584 | bytes 22643200 | tf_op jit(solution)/shard_map/dot_general | solution.py:464
  206.0 11.1 %fusion.5.x_ref = f32[4,4096]{1,0:T(4,128)} fusion(bf16[4,2752]{1,0:T(4,128)(2,1)S(1)} %fusion.22, bf16[1,2752,4096]{2,1,0:T(8,128)(2,1)} %param.38), kind=kOutput, calls=%fused_computation.23 | convolution fusion | flops 90177536 | bytes 22631936 | tf_op jit(solution)/shard_map/dot_general | solution.py:466
  217.1 6.8 %share12.1 = f32[4,4096]{1,0:T(4,128)} custom-call(f32[4,4096]{1,0:T(4,128)} %fusion.5.x_ref), custom_call_target="tpu_custom_call" | custom-call | tf_op jit(solution)/shard_map/share12/pallas_call | solution.py:402
  224.0 1.0 multiply_reduce_fusion
  225.0 25.1 %fusion.72 = (f32[4]{0:T(128)S(1)}, f32[4,8000]{1,0:T(4,128)S(1)}) fusion(bf16[4096,8000]{0,1:T(8,128)(2,1)} %param.40, f32[4096]{0:T(1024)S(1)} %convert_element_type.49, f32[4]{0:T(128)S(1)} %add_rsqrt_fusion, f32[4,4096]{1,0:T(4,128)} %share12.1, f32[4,4096]{1,0:T(4,128)S(1)} %copy-done.5, bf16[4,4096]{1,0:T(4,128)(2,1)S(1)} %copy-done.4), kind=kOutput, calls=%fused_computation.118 | convolution fusion | flops 262274304 | bytes 65844256 | tf_op jit(solution)/shard_map/dot_general | solution.py:467
  251.1 5.3 %share13.1 = f32[4,8,128]{2,1,0:T(8,128)} custom-call(f32[8,128]{1,0:T(8,128)} %broadcast.387.x_ref), custom_call_target="tpu_custom_call" | custom-call | tf_op jit(solution)/shard_map/share13/pallas_call | solution.py:402
  257.3 1.0 multiply_reduce_fusion.2
  258.9 9.7 %share10.1 = f32[8,4,128]{2,1,0:T(4,128)} custom-call(f32[4,128]{1,0:T(4,128)} %broadcast_in_dim.129.x_ref), custom_call_target="tpu_custom_call" | custom-call | tf_op jit(solution)/shard_map/share10/pallas_call | solution.py:402
  268.8 1.4 gather_fusion.2
  (42 shorter events, 4.2 us)
Async XLA Ops:
  0.6 4.6 %copy-start.3 = (bf16[1,4,512,8,128]{4,3,2,1,0:T(8,128)(2,1)S(1)}, bf16[1,4,512,8,128]{4,3,2,1,0:T(8,128)(2,1)}, u32[]{:S(2)}) copy-start(bf16[1,4,512,8,128]{4,3,2,1,0:T(8,128)(2,1)} %param.29) | copy-start | bytes 12582916
  5.2 2.0 copy-start.9
  15.0 96.7 %copy-start.6 = (bf16[1,4096]{1,0:T(2,128)(2,1)S(1)}, bf16[1,4096]{1,0:T(2,128)(2,1)}, u32[]{:S(2)}) copy-start(bf16[1,4096]{1,0:T(2,128)(2,1)} %param.30) | copy-start | bytes 24580
  15.0 96.7 %copy-start.4 = (bf16[4,4096]{1,0:T(4,128)(2,1)S(1)}, bf16[4,4096]{1,0:T(4,128)(2,1)}, u32[]{:S(2)}) copy-start(bf16[4,4096]{1,0:T(4,128)(2,1)} %param.24) | copy-start | bytes 98308
  100.1 4.6 %copy-start = (bf16[4,4096,128]{2,1,0:T(8,128)(2,1)S(1)}, bf16[4,4096,128]{2,1,0:T(8,128)(2,1)}, u32[]{:S(2)}) copy-start(bf16[4,4096,128]{2,1,0:T(8,128)(2,1)} %get-tuple-element.483) | copy-start | bytes 12582916 | tf_op jit(solution)/shard_map/cond
  150.7 6.5 %copy-start.8 = (bf16[4096]{0:T(1024)(128)(2,1)S(1)}, bf16[4096]{0:T(1024)(128)(2,1)}, u32[]{:S(2)}) copy-start(bf16[4096]{0:T(1024)(128)(2,1)} %param.39) | copy-start | bytes 24580
  150.7 6.4 %copy-start.7 = (bf16[1,4096]{1,0:T(2,128)(2,1)S(1)}, bf16[1,4096]{1,0:T(2,128)(2,1)}, u32[]{:S(2)}) copy-start(bf16[1,4096]{1,0:T(2,128)(2,1)} %param.35) | copy-start | bytes 24580
  206.0 18.0 %copy-start.5 = (f32[4,4096]{1,0:T(4,128)S(1)}, f32[4,4096]{1,0:T(4,128)}, u32[]{:S(2)}) copy-start(f32[4,4096]{1,0:T(4,128)} %share11.1) | copy-start | bytes 196612
  225.0 33.3 %copy-start.10 = (f32[4]{0:T(128)S(1)}, f32[4]{0:T(128)}, u32[]{:S(2)}) copy-start(f32[4]{0:T(128)} %param.27) | copy-start | bytes 52
